TPU v7x, 128 devices: a whole 4x4x4 slice. The times are simulated.
128 devices in a mesh: enc: 8 (over z, core), ctx: 16 (over y, x).
Axes of the slice: x: 4, y: 4, z: 4, core: 2. Of those that a mesh axis runs over, the one named last changes fastest.
Arguments:
- patches: bfloat16 [6144, 1280], P('enc'), may hold values from -17 to 17
- patch_image: int32 [6144], P('enc'), may hold values from 63 to 1535, as said below
- vit_gain: float32 [1280], replicated, may hold values from 0.1 to 1.9
- vit_qkv: bfloat16 [1280, 16, 240], P(None, 'ctx')
- vit_proj: bfloat16 [1280, 1280], P('ctx'), may hold values from -0.15625 to 0.15625
- merge_gain: float32 [1280], replicated, may hold values from 0.1 to 1.9
- merge_up: bfloat16 [5120, 5120], P(None, 'ctx'), may hold values from -0.078125 to 0.078125
- merge_down: bfloat16 [5120, 8192], P('ctx', 'enc'), may hold values from -0.078125 to 0.078125
- text_embed: bfloat16 [6144, 8192], P('ctx', 'enc'), may hold values from -17 to 17
- placeholder_unit: int32 [6144], replicated, may hold values from -1 to 1535, as said below
- doc_id: int32 [6144], replicated, may hold values from 0 to 31, never falling along the last dimension, each value on 1 to 3456 neighbouring positions
- dec_gain: float32 [8192], replicated, may hold values from 0.1 to 1.9
- dec_wq: bfloat16 [8192, 4096], P(None, 'enc')
- dec_wk: bfloat16 [8192, 1024], P(None, 'enc')
- dec_wv: bfloat16 [8192, 1024], P(None, 'enc'), may hold values from -0.0625 to 0.0625
Outputs:
- attended: bfloat16 [6144, 4096], P('ctx', 'enc')
Inputs may be any that keep to these rules, and one draw needn't show every extreme that they name: `patch_image`: the patches of an image are consecutive, start at a multiple of 4, number a multiple of 4 and at most 256, and lie within one aligned block of 768 patches; image numbers never fall and differ between images; in every such block some image has exactly 256 patches. `placeholder_unit`: -1 marks a text position. Every unit appears exactly once; the units of one image fill consecutive placeholders in their order; the placeholders of an aligned block of 384 positions are consecutive and number at most 192, and some block holds exactly 192. `doc_id`: document numbers never fall; a document has at most 3456 positions, and some document exactly 3456.
All inputs are finite; a program needn't handle non-finite values.
Results may differ from a plain program's by a relative error of at most 0.0085.
Values may be sent and summed in bfloat16 or wider, within the bound.
A program may use at most 128 MiB of HBM per device.

v0:
```python
import math
import jax
import jax.numpy as jnp
from jax import lax
from jax.sharding import PartitionSpec as P

HD = 128
QPK = 4
EPSILON = 1e-06
NEGATIVE = -1e30


def in_blocks(x, dim, size):
    dims = x.shape
    blocks = x.reshape(*dims[:dim], size, dims[dim] // size, *dims[dim + 1 :])
    return jnp.moveaxis(blocks, dim, 0)


def sent_and_summed(x, axis, dim):
    blocks = in_blocks(x, dim, lax.axis_size(axis))
    arrived = lax.all_to_all(blocks, axis, split_axis=0, concat_axis=0, tiled=True)
    return arrived.sum(axis=0)


def in_order(blocks, dim):
    dims = list(blocks.shape[1:])
    dims[dim] *= blocks.shape[0]
    return jnp.moveaxis(blocks, 0, dim).reshape(dims)


def sent_to_all(x, axis):
    size = lax.axis_size(axis)
    return lax.all_to_all(jnp.broadcast_to(x[None], (size, *x.shape)), axis, 0, 0, tiled=True)


def gathered_copies(x, axis, dim):
    return in_order(sent_to_all(x, axis), dim)


def of_everyone(x, axis):
    return sent_to_all(x, axis).sum(axis=0)


def in_one_piece(arrays, axis, dim, along):
    widths = [a.shape[along] for a in arrays]
    both = jnp.concatenate(arrays, axis=along)
    result = lax.all_gather(both, axis, axis=dim, tiled=True)
    return tuple(jnp.split(result, [sum(widths[:k]) for k in range(1, len(widths))], axis=along))


def layer_norm(values, scaling):
    widened = values.astype(jnp.float32)
    center = widened - jnp.mean(widened, axis=1, keepdims=True)
    spread = jnp.mean(center * center, axis=1, keepdims=True)
    return (center * lax.rsqrt(spread + EPSILON) * scaling).astype(jnp.bfloat16)


def image_attention(queries, keys_in, values_in, image_ids):
    head_count, row_count, head_width = queries.shape
    block_rows = math.gcd(row_count, 512)
    scaling = head_width ** (-0.5)

    def image_one_block(offset):
        query_block = lax.dynamic_slice_in_dim(queries, offset, block_rows, 1)
        block_ids = lax.dynamic_slice_in_dim(image_ids, offset, block_rows, 0)
        allowed = block_ids[:, None] == image_ids[None, :]
        scores = (
            jnp.einsum("hqd,hkd->hqk", query_block, keys_in, preferred_element_type=jnp.float32)
            * scaling
        )
        scores = jnp.where(allowed[None], scores, NEGATIVE)
        highest = jnp.max(scores, axis=2, keepdims=True)
        weights = jnp.exp(scores - highest)
        totals = jnp.sum(weights, axis=2, keepdims=True)
        mixture = jnp.einsum(
            "hqk,hkd->hqd",
            weights.astype(jnp.bfloat16),
            values_in,
            preferred_element_type=jnp.float32,
        )
        return (mixture / totals).astype(jnp.bfloat16)

    offsets = jnp.arange(row_count // block_rows, dtype=jnp.int32) * block_rows
    blocks = lax.map(image_one_block, offsets)
    return blocks.transpose(1, 0, 2, 3).reshape(head_count, row_count, head_width)


def body(
    patches,
    patch_image,
    vit_gain,
    vit_qkv,
    vit_proj,
    merge_gain,
    merge_up,
    merge_down,
    text_embed,
    placeholder_unit,
    doc_id,
    dec_gain,
    dec_wq,
    dec_wk,
    dec_wv,
):
    ctx_count = lax.axis_size("ctx")
    enc_count = lax.axis_size("enc")
    ctx_index = lax.axis_index("ctx")
    group_rows = patches.shape[0]
    head_count = vit_qkv.shape[1]
    head_width = vit_qkv.shape[2] // 3
    normed_patches = layer_norm(patches, vit_gain)
    packed = jnp.dot(
        normed_patches,
        vit_qkv.reshape(vit_qkv.shape[0], head_count * 3 * head_width),
        preferred_element_type=jnp.float32,
    )
    packed = (
        packed.astype(jnp.bfloat16)
        .reshape(group_rows, head_count, 3, head_width)
        .transpose(2, 1, 0, 3)
    )
    attended_patches = image_attention(packed[0], packed[1], packed[2], patch_image)
    flat_heads = attended_patches.transpose(1, 0, 2).reshape(group_rows, head_count * head_width)
    head_terms = jnp.dot(flat_heads, vit_proj, preferred_element_type=jnp.float32)
    share_sum = sent_and_summed(head_terms, "ctx", 0)
    share_count = share_sum.shape[0]
    own_rows = lax.dynamic_slice_in_dim(patches, ctx_index * share_count, share_count, 0)
    own_out = (own_rows.astype(jnp.float32) + share_sum).astype(jnp.bfloat16)
    own_normed = layer_norm(lax.optimization_barrier(own_out), merge_gain)
    merge_input = gathered_copies(own_normed, "ctx", 0)
    unit_inputs = merge_input.reshape(group_rows // 4, 4 * merge_input.shape[1])
    hidden = jax.nn.gelu(
        jnp.dot(unit_inputs, merge_up, preferred_element_type=jnp.float32), approximate=False
    ).astype(jnp.bfloat16)
    all_hidden = gathered_copies(hidden, "enc", 0)
    unit_total = all_hidden.shape[0]
    tok_rows = text_embed.shape[0]
    feature_cols = text_embed.shape[1]
    local_units = lax.dynamic_slice_in_dim(placeholder_unit, ctx_index * tok_rows, tok_rows, 0)
    present = local_units >= 0
    slot_rows = tok_rows // 2
    shard_units = placeholder_unit.reshape(ctx_count, tok_rows)
    shard_present = shard_units >= 0
    shard_rank = jnp.cumsum(shard_present.astype(jnp.int32), axis=1) - 1
    matches = shard_present[:, None, :] & (
        shard_rank[:, None, :] == jnp.arange(slot_rows, dtype=jnp.int32)[None, :, None]
    )
    slot_units = (jnp.sum(jnp.where(matches, shard_units[:, None, :] + 1, 0), axis=2) - 1).reshape(
        -1
    )
    picked = jnp.take(all_hidden, jnp.clip(slot_units, 0, unit_total - 1), axis=0)
    picked = jnp.where((slot_units >= 0)[:, None], picked, jnp.zeros_like(picked))
    arrived = lax.psum_scatter(
        jnp.dot(picked, merge_down, preferred_element_type=jnp.float32),
        "ctx",
        scatter_dimension=0,
        tiled=True,
    ).astype(jnp.bfloat16)
    local_rank = jnp.cumsum(present.astype(jnp.int32)) - 1
    vision_local = jnp.take(arrived, jnp.clip(local_rank, 0, slot_rows - 1), axis=0)
    sequence = jnp.where(present[:, None], vision_local, text_embed)
    local_wide = sequence.astype(jnp.float32)
    squares = of_everyone(jnp.sum(local_wide * local_wide, axis=1), "enc")
    row_scale = lax.rsqrt(squares / (feature_cols * enc_count) + EPSILON)
    start_state = (
        jnp.zeros((tok_rows, dec_wq.shape[1]), jnp.float32),
        jnp.zeros((tok_rows, dec_wk.shape[1]), jnp.float32),
        jnp.zeros((tok_rows, dec_wv.shape[1]), jnp.float32),
    )
    normed_part = (
        lax.all_gather(sequence, "enc", axis=1, tiled=True).astype(jnp.float32)
        * row_scale[:, None]
        * dec_gain
    ).astype(jnp.bfloat16)
    query_part = jnp.dot(normed_part, dec_wq, preferred_element_type=jnp.float32)
    key_part = jnp.dot(normed_part, dec_wk, preferred_element_type=jnp.float32)
    value_part = jnp.dot(normed_part, dec_wv, preferred_element_type=jnp.float32)
    queries_flat = query_part.astype(jnp.bfloat16)
    keys_local = key_part.astype(jnp.bfloat16)
    values_local = value_part.astype(jnp.bfloat16)
    kv_local = dec_wk.shape[1] // HD
    queries = queries_flat.reshape(tok_rows, kv_local, QPK, HD).transpose(1, 2, 0, 3)
    query_first = ctx_index * tok_rows
    query_pos = query_first + jnp.arange(tok_rows, dtype=jnp.int32)
    query_docs = lax.dynamic_slice_in_dim(doc_id, query_first, tok_rows, 0)
    scaling = HD ** (-0.5)
    start_state = (
        jnp.full((kv_local, QPK, tok_rows), NEGATIVE, jnp.float32),
        jnp.zeros((kv_local, QPK, tok_rows), jnp.float32),
        jnp.zeros((kv_local, QPK, tok_rows, HD), jnp.float32),
    )
    offset = jnp.int32(0)
    key_part, value_part = in_one_piece((keys_local, values_local), "ctx", 0, 1)
    key_count = key_part.shape[0]
    sub_rows = math.gcd(key_count, 512)
    last_doc = lax.dynamic_slice_in_dim(doc_id, offset + key_count - 1, 1, 0)[0]
    visible = (offset <= query_first + tok_rows - 1) & (last_doc >= query_docs[0])

    def update(current):

        def update_one_block(turn_index, inner_state):
            highest, totals, mixture = inner_state
            begin_row = turn_index * sub_rows
            keys_block = lax.dynamic_slice_in_dim(key_part, begin_row, sub_rows, 0).reshape(
                sub_rows, kv_local, HD
            )
            values_block = lax.dynamic_slice_in_dim(value_part, begin_row, sub_rows, 0).reshape(
                sub_rows, kv_local, HD
            )
            key_pos = begin_row + jnp.arange(sub_rows, dtype=jnp.int32)
            key_docs = lax.dynamic_slice_in_dim(doc_id, begin_row, sub_rows, 0)
            allowed = (key_pos[None, :] <= query_pos[:, None]) & (
                key_docs[None, :] == query_docs[:, None]
            )
            scores = (
                jnp.einsum(
                    "gjtd,sgd->gjts", queries, keys_block, preferred_element_type=jnp.float32
                )
                * scaling
            )
            new_peak = jnp.maximum(highest, jnp.max(jnp.where(allowed, scores, NEGATIVE), axis=3))
            factor = jnp.exp(highest - new_peak)
            weights = jnp.where(allowed, jnp.exp(scores - new_peak[..., None]), 0.0)
            totals = totals * factor + jnp.sum(weights, axis=3)
            mixture = mixture * factor[..., None] + jnp.einsum(
                "gjts,sgd->gjtd",
                weights.astype(jnp.bfloat16),
                values_block,
                preferred_element_type=jnp.float32,
            )
            return (new_peak, totals, mixture)

        return lax.fori_loop(0, key_count // sub_rows, update_one_block, current)

    def unchanged(current):
        return current

    finished = lax.cond(visible, update, unchanged, start_state)
    outputs = (finished[2] / finished[1][..., None]).astype(jnp.bfloat16)
    return outputs.transpose(2, 0, 1, 3).reshape(tok_rows, kv_local * QPK * HD)


def solution(mesh):
    placed = (
        P("enc", None),
        P("enc"),
        P(),
        P(None, "ctx", None),
        P("ctx", None),
        P(),
        P(None, "ctx"),
        P("ctx", "enc"),
        P("ctx", "enc"),
        P(),
        P(),
        P(),
        P(None, "enc"),
        P(None, "enc"),
        P(None, "enc"),
    )
    return jax.shard_map(
        body, mesh=mesh, in_specs=placed, out_specs=P("ctx", "enc"), check_vma=False
    )
```

profile of v0, /device:TPU:0, one launch (start us, length us, event | category | flops | bytes accessed | tf_op | source)
XLA Modules:
  0.0 493.8 jit_solution(5505292122462072174)
XLA Ops:
  6.6 2.0 convert_reduce_fusion
  11.3 2.0 copy.40
  13.3 1.9 slice_bitcast_fusion
  15.2 16.2 %while.28 = (s32[]{:T(128)}, bf16[3,1,256,80]{2,3,1,0:T(8,128)(2,1)}, s32[3]{0:T(128)S(1)}, s32[768]{0:T(1024)S(1)}, bf16[1,768,80]{2,1,0:T(8,128)(2,1)}, /*inde...) while((s32[]{:T(128)}, ...), condition=%wide.region_10.11_spmd, body=%wide.region_7.10_spmd.sunk | while | flops 64527876 | bytes 2797211 | solution.py:84
  32.5 3.5 fusion.79
  36.0 7.2 %all-to-all-start = ((f32[16,48,1280]{2,1,0:T(8,128)}), f32[16,48,1280]{2,1,0:T(8,128)}, u32[]{:S(2)}, u32[]{:S(2)}) async-start(f32[16,48,1280]{2,1,0:T(8,128)} %fusion.79), calls=%async_computation | async-start | bytes 7864320 | tf_op jit(solution)/shard_map/all_to_all | solution.py:21
  43.2 59.5 %all-to-all-done = f32[16,48,1280]{2,1,0:T(8,128)} async-done(((f32[16,48,1280]{2,1,0:T(8,128)}), f32[16,48,1280]{2,1,0:T(8,128)}, u32[]{:S(2)}, u32[]{:S(2)}) %all-to-all-start) | async-done | bytes 3932192 | tf_op jit(solution)/shard_map/all_to_all | solution.py:21
  102.7 2.3 reduce_sum.97
  107.9 4.5 all-to-all-start.1
  115.6 24.9 %all-to-all-done.1 = bf16[16,48,1280]{2,1,0:T(8,128)(2,1)} async-done(((bf16[16,48,1280]{2,1,0:T(8,128)(2,1)}), bf16[16,48,1280]{2,1,0:T(8,128)(2,1)}, u32[]{:S(2)}, u32[]{:S(2)}) %all-to-all-start.1) | async-done | bytes 1966112 | tf_op jit(solution)/shard_map/all_to_all | solution.py:33
  140.5 4.1 reshape_reshape.3
  144.6 3.6 fusion.66
  149.3 5.3 %all-to-all-start.2 = ((bf16[8,192,320]{2,1,0:T(8,128)(2,1)}), bf16[8,192,320]{2,1,0:T(8,128)(2,1)S(1)}, u32[]{:S(2)}, u32[]{:S(2)}) async-start(bf16[8,192,320]{2,1,0:T(8,128)(2,1)} %broadcast_in_dim.158), calls=%async_computation.2 | async-start | bytes 2359296 | tf_op jit(solution)/shard_map/all_to_all | solution.py:33
  154.7 17.3 %all-to-all-done.2 = bf16[8,192,320]{2,1,0:T(8,128)(2,1)S(1)} async-done(((bf16[8,192,320]{2,1,0:T(8,128)(2,1)}), bf16[8,192,320]{2,1,0:T(8,128)(2,1)S(1)}, u32[]{:S(2)}, u32[]{:S(2)}) %all-to-all-start.2) | async-done | bytes 983072 | tf_op jit(solution)/shard_map/all_to_all | solution.py:33
  171.9 11.0 %gather_fusion = bf16[3072,320]{1,0:T(8,128)(2,1)S(1)} fusion(bf16[1536,320]{1,0:T(8,128)(2,1)S(1)} %bitcast.146, s32[3072]{0:T(1024)S(1)} %broadcast_clamp_fusion), kind=kCustom, calls=%fused_computation | custom fusion | bytes 3944448 | tf_op jit(solution)/shard_map/jit(_take)/gather | solution.py:151
  182.9 7.6 %fusion.47 = f32[3072,1024]{1,0:T(8,128)} fusion(bf16[320,1024]{1,0:T(8,128)(2,1)} %param.28, bf16[3072,320]{1,0:T(8,128)(2,1)S(1)} %gather_fusion, pred[3072]{0:T(1024)(128)(4,1)} %compare_and_fusion.1, pred[3072]{0:T(1024)(128)(4,1)S(1)} %ge.77), kind=kOutput, calls=%fused_computation.61 | convolution fusion | flops 2015232000 | bytes 15210496 | tf_op jit(solution)/shard_map/dot_general | solution.py:154
  192.2 88.8 %reduce-scatter.2.cloned.1.call-done = f32[192,1024]{1,0:T(8,128)} async-done(((f32[3072,1024]{1,0:T(8,128)}), f32[192,1024]{1,0:T(8,128)}) %reduce-scatter.2.cloned.1.call-update) | async-done | bytes 786448 | tf_op jit(solution)/shard_map/reduce_scatter | solution.py:153
  282.2 2.1 gather_fusion.1
  285.7 9.6 %all_to_all.21 = f32[8,1,384]{2,1,0:T(1,128)S(1)} all-to-all(f32[8,1,384]{2,1,0:T(1,128)S(1)} %broadcast_in_dim.162), channel_id=1, replica_groups=mesh['enc'=8,'ctx'=16] {'enc'}, dimensions={0} | all-to-all | bytes 24576 | tf_op jit(solution)/shard_map/all_to_all | solution.py:33
  295.3 30.6 %all-gather.3.cloned.1.call-done = bf16[384,8192]{1,0:T(8,128)(2,1)} async-done(((bf16[384,1024]{1,0:T(8,128)(2,1)}), bf16[384,8192]{1,0:T(8,128)(2,1)}) %all-gather.3.cloned.1.call-update) | async-done | bytes 6291472 | tf_op jit(solution)/shard_map/all_gather | solution.py:171
  325.9 5.7 %convolution_convert_fusion.2 = bf16[384,128]{0,1:T(8,128)(2,1)S(1)} fusion(bf16[8192,128]{1,0:T(8,128)(2,1)} %param.34, bf16[384,8192]{1,0:T(8,128)(2,1)} %all-gather.3.cloned.1.call-done, f32[8192]{0:T(1024)S(1)} %copy-done.10, f32[384]{0:T(512)S(1)} %add_rsqrt_fusion.1), kind=kOutput, calls=%fused_computation.76 | convolution fusion | flops 817938432 | bytes 8521216 | tf_op jit(solution)/shard_map/dot_general | solution.py:176
  331.7 2.2 convolution_convert_fusion.1
  338.5 8.7 %convolution_convert_fusion = bf16[384,512]{1,0:T(8,128)(2,1)S(1)} fusion(bf16[8192,512]{1,0:T(8,128)(2,1)} %param.33, bf16[384,8192]{1,0:T(8,128)(2,1)} %all-gather.3.cloned.1.call-done, f32[8192]{0:T(1024)S(1)} %copy-done.10, f32[384]{0:T(512)S(1)} %add_rsqrt_fusion.1), kind=kOutput, calls=%fused_computation.71 | convolution fusion | flops 3234004992 | bytes 15107584 | tf_op jit(solution)/shard_map/dot_general | solution.py:175
  348.1 38.2 %all-gather.5.cloned.1.call-done = bf16[6144,256]{0,1:T(8,128)(2,1)} async-done(((bf16[384,256]{0,1:T(8,128)(2,1)}), bf16[6144,256]{0,1:T(8,128)(2,1)}) %all-gather.5.cloned.1.call-update) | async-done | bytes 3145744 | tf_op jit(solution)/shard_map/all_gather | solution.py:47
  386.4 98.2 %conditional.1 = (f32[1,4,384]{2,1,0:T(4,128)}, f32[1,4,384,128]{3,2,1,0:T(8,128)}) conditional(s32[]{:T(128)} %convert_element_type.75, () %tuple.31, (bf16[6144,256]{0,1:T(8,128)(2,1)}, s32[]{:T(128)}, s32[384]{0:T(512)S(1)}, s32[6144]{0:T(1024)}, s32[384]{0:T(512)S(1)}, /*index=5*/bf16[1,4,384,128]{3,2,1,0:T(8,128)(2,1)}) %tuple.87), branch_computations={%region_17.18_spmd, %region_18.23_spmd} | conditional | flops 412493696 | bytes 25149788 | solution.py:238
  386.4 3.2 copy.44
  389.5 1.9 fusion.87
  391.4 93.2 %while.27 = (s32[]{:T(128)}, f32[1,4,384]{2,1,0:T(4,128)S(1)}, f32[1,4,384]{2,1,0:T(4,128)}, f32[1,4,384,128]{3,2,1,0:T(8,128)}, s32[384]{0:T(512)S(1)}, /*index...) while((s32[]{:T(128)}, f32[1,4,384]{2,1,0:T(4,128)S(1)}, ...), condition=%wide.region_22.22_spmd.clone, body=%wide.region_19.21_spmd.clone.sunk | while | flops 412493312 | bytes 12563663 | solution.py:233
  394.2 2.8 fusion.116
  401.0 3.1 fusion.116
  408.9 3.1 fusion.116
  416.7 3.1 fusion.116
  422.8 1.7 fusion.113
  424.6 3.1 fusion.116
  430.6 1.7 fusion.113
  432.4 3.1 fusion.116
  438.5 1.7 fusion.113
  440.3 3.1 fusion.116
  446.3 1.7 fusion.113
  448.1 3.1 fusion.116
  454.2 1.7 fusion.113
  456.0 3.1 fusion.116
  462.0 1.7 fusion.113
  463.8 3.1 fusion.116
  469.9 1.7 fusion.113
  471.7 3.1 fusion.116
  477.7 1.7 fusion.113
  479.5 3.1 fusion.116
  (195 shorter events, 73.9 us)
Async XLA Ops:
  6.5 138.1 %copy-start = (bf16[5120,320]{0,1:T(8,128)(2,1)S(1)}, bf16[5120,320]{0,1:T(8,128)(2,1)}, u32[]{:S(2)}) copy-start(bf16[5120,320]{0,1:T(8,128)(2,1)} %param.27) | copy-start | bytes 9830404
  6.5 3.0 copy-start.11
  6.5 2.3 copy-start.2
  6.5 3.0 copy-start.9
  9.5 5.7 %copy-start.6 = (s32[768]{0:T(1024)S(1)}, s32[768]{0:T(1024)}, u32[]{:S(2)}) copy-start(s32[768]{0:T(1024)} %param.22) | copy-start | bytes 9220
  36.0 66.7 %all-to-all-start = ((f32[16,48,1280]{2,1,0:T(8,128)}), f32[16,48,1280]{2,1,0:T(8,128)}, u32[]{:S(2)}, u32[]{:S(2)}) async-start(f32[16,48,1280]{2,1,0:T(8,128)} %fusion.79), calls=%async_computation | async-start | bytes 7864320 | tf_op jit(solution)/shard_map/all_to_all | solution.py:21
  43.2 63.2 %copy-start.5 = (f32[1280]{0:T(1024)S(1)}, f32[1280]{0:T(1024)}, u32[]{:S(2)}) copy-start(f32[1280]{0:T(1024)} %param.26) | copy-start | bytes 15364
  106.3 6.0 %copy-start.4 = (s32[6144]{0:T(1024)S(1)}, s32[6144]{0:T(1024)}, u32[]{:S(2)}) copy-start(s32[6144]{0:T(1024)} %param.30) | copy-start | bytes 73732
  107.9 32.7 %all-to-all-start.1 = ((bf16[16,48,1280]{2,1,0:T(8,128)(2,1)}), bf16[16,48,1280]{2,1,0:T(8,128)(2,1)}, u32[]{:S(2)}, u32[]{:S(2)}) async-start(bf16[16,48,1280]{2,1,0:T(8,128)(2,1)} %broadcast_in_dim.157), calls=%async_computation.1 | async-start | bytes 3932160 | tf_op jit(solution)/shard_map/all_to_all | solution.py:33
  149.3 22.6 %all-to-all-start.2 = ((bf16[8,192,320]{2,1,0:T(8,128)(2,1)}), bf16[8,192,320]{2,1,0:T(8,128)(2,1)S(1)}, u32[]{:S(2)}, u32[]{:S(2)}) async-start(bf16[8,192,320]{2,1,0:T(8,128)(2,1)} %broadcast_in_dim.158), calls=%async_computation.2 | async-start | bytes 2359296 | tf_op jit(solution)/shard_map/all_to_all | solution.py:33
  154.6 126.4 %reduce-scatter.2.cloned.1.call-start = ((), (), s32[]{:S(2)}) async-start(), calls=%async_computation.5 | async-start | bytes 13369344 | tf_op jit(solution)/shard_map/reduce_scatter | solution.py:153
  190.6 135.3 %all-gather.3.cloned.1.call-start = ((), (), s32[]{:S(2)}) async-start(), calls=%async_computation.6 | async-start | bytes 7077888 | tf_op jit(solution)/shard_map/all_gather | solution.py:171
  282.1 2.1 copy-start.3
  284.2 41.7 %copy-start.10 = (f32[8192]{0:T(1024)S(1)}, f32[8192]{0:T(1024)}, u32[]{:S(2)}) copy-start(f32[8192]{0:T(1024)} %param.32) | copy-start | bytes 98308
  285.6 100.7 %all-gather.5.cloned.1.call-start = ((), (), s32[]{:S(2)}) async-start(), calls=%async_computation.7 | async-start | bytes 3342336 | tf_op jit(solution)/shard_map/all_gather | solution.py:47
  295.3 36.3 %copy-start.8 = (bf16[8192,128]{1,0:T(8,128)(2,1)S(1)}, bf16[8192,128]{1,0:T(8,128)(2,1)}, u32[]{:S(2)}) copy-start(bf16[8192,128]{1,0:T(8,128)(2,1)} %param.35) | copy-start | bytes 6291460
  325.9 5.7 %copy-start.7 = (bf16[384,8192]{1,0:T(8,128)(2,1)S(1)}, bf16[384,8192]{1,0:T(8,128)(2,1)}, u32[]{:S(2)}) copy-start(bf16[384,8192]{1,0:T(8,128)(2,1)} %all-gather.3.cloned.1.call-done) | copy-start | bytes 18874372
  484.6 2.7 copy-start.1
Sparse Core Ops, SparseCore 0:
  190.7 90.2 reduce-scatter.1
  285.8 40.1 all-gather.2
  334.7 51.5 all-gather.4
where the time goes:
time: 496 us; the launch traced here: 494 us
  waiting for transfers between devices  259 us (52%)
  matrix products  97.8 us (20%)
  local copies, waits for them, and re-layouts  46.6 us (9%)
  other arithmetic  41.9 us (8%)
  starting transfers between devices  17.1 us (3%)
  between operations  14.8 us (3%)
  blocking collectives  9.58 us (2%)
  loops' own time  6.57 us (1%)
    reduce_scatter x1, waiting for transfers between devices, body(): lax.psum_scatter(jnp.dot(picked, merge_down, preferred_element_type=jnp.f...  88.8 us
    all_to_all x1, waiting for transfers between devices, sent_and_summed(): lax.all_to_all(blocks, axis, split_axis=0, concat_axis=0, tiled=True)  59.5 us
    all_to_all x2, waiting for transfers between devices, sent_to_all(): lax.all_to_all(jnp.broadcast_to(x[None], (size, *x.shape)), axis, 0, 0, t...  42.2 us
    all_gather x1, waiting for transfers between devices, in_one_piece(): result = lax.all_gather(both, axis, axis=dim, tiled=True)  38.2 us
    dot_general x12, matrix products, update_one_block(): jnp.einsum('gjts,sgd->gjtd', weights.astype(jnp.bfloat16), values_block,...  36.9 us
    all_gather x1, waiting for transfers between devices, body(): lax.all_gather(sequence, 'enc', axis=1, tiled=True).astype(jnp.float32)  30.6 us
    dot_general x12, matrix products, update_one_block(): jnp.einsum('gjtd,sgd->gjts', queries, keys_block, preferred_element_type=...  20.9 us
    add x12, other arithmetic, update_one_block(): totals = totals * factor + jnp.sum(weights, axis=3)  14.8 us
  transfers between devices with their start and end apart: 6, of which 6 were waited for; matrix products, arithmetic and copies ran while one was open for 3% of the time, Pallas kernels for 0%

commit v1 on v0

--- a/solution.py
+++ b/solution.py
@@ -8,6 +8,14 @@
 QPK = 4
 EPSILON = 1e-06
 NEGATIVE = -1e30
+
+
+def gather_by_exchange(shard, axis, dim):
+    peers = lax.axis_size(axis)
+    repeats = [peers if d == dim else 1 for d in range(shard.ndim)]
+    return lax.all_to_all(
+        jnp.tile(shard, repeats), axis, split_axis=dim, concat_axis=dim, tiled=True
+    )
 
 
 def in_blocks(x, dim, size):
@@ -168,9 +176,7 @@
         jnp.zeros((tok_rows, dec_wv.shape[1]), jnp.float32),
     )
     normed_part = (
-        lax.all_gather(sequence, "enc", axis=1, tiled=True).astype(jnp.float32)
-        * row_scale[:, None]
-        * dec_gain
+        gather_by_exchange(sequence, "enc", 1).astype(jnp.float32) * row_scale[:, None] * dec_gain
     ).astype(jnp.bfloat16)
     query_part = jnp.dot(normed_part, dec_wq, preferred_element_type=jnp.float32)
     key_part = jnp.dot(normed_part, dec_wk, preferred_element_type=jnp.float32)

time: 496 us -> 553 us (1.11)
  waiting for transfers between devices: 259 us -> 298 us
  local copies, waits for them, and re-layouts: 46.6 us -> 60.5 us
    all_to_all x0 -> x1, waiting for transfers between devices: none -> 72 us  [gather_by_exchange(): lax.all_to_all(jnp.tile(shard, repeats), axis, split_axis=dim, concat_axi...]
    all_gather x1 -> x0, waiting for transfers between devices: 30.6 us -> none  [body(): lax.all_gather(sequence, 'enc', axis=1, tiled=True).astype(jnp.float32)]
    all_to_all x0 -> x1, local copies, waits for them, and re-layouts: none -> 8.63 us  [gather_by_exchange(): lax.all_to_all(jnp.tile(shard, repeats), axis, split_axis=dim, concat_axi...]
    convert_element_type x0 -> x1, other arithmetic: none -> 5.61 us  [body(): normed_part = (gather_by_exchange(sequence, 'enc', 1).astype(jnp.float32)...]
where the time goes in v1:
time: 553 us; the launch traced here: 551 us
  waiting for transfers between devices  298 us (54%)
  matrix products  92.7 us (17%)
  local copies, waits for them, and re-layouts  60.5 us (11%)
  other arithmetic  46.7 us (8%)
  starting transfers between devices  21.8 us (4%)
  between operations  15.1 us (3%)
  blocking collectives  9.58 us (2%)
  loops' own time  6.57 us (1%)
    reduce_scatter x1, waiting for transfers between devices, body(): lax.psum_scatter(jnp.dot(picked, merge_down, preferred_element_type=jnp.f...  88.8 us
    all_to_all x1, waiting for transfers between devices, gather_by_exchange(): lax.all_to_all(jnp.tile(shard, repeats), axis, split_axis=dim, concat_axi...  72 us
    all_to_all x1, waiting for transfers between devices, sent_and_summed(): lax.all_to_all(blocks, axis, split_axis=0, concat_axis=0, tiled=True)  59.5 us
    all_to_all x2, waiting for transfers between devices, sent_to_all(): lax.all_to_all(jnp.broadcast_to(x[None], (size, *x.shape)), axis, 0, 0, t...  42.2 us
    dot_general x12, matrix products, update_one_block(): jnp.einsum('gjts,sgd->gjtd', weights.astype(jnp.bfloat16), values_block,...  36.9 us
    all_gather x1, waiting for transfers between devices, in_one_piece(): result = lax.all_gather(both, axis, axis=dim, tiled=True)  35.1 us
    dot_general x12, matrix products, update_one_block(): jnp.einsum('gjtd,sgd->gjts', queries, keys_block, preferred_element_type=...  20.9 us
    add x12, other arithmetic, update_one_block(): totals = totals * factor + jnp.sum(weights, axis=3)  14.8 us
  transfers between devices with their start and end apart: 6, of which 6 were waited for; matrix products, arithmetic and copies ran while one was open for 3% of the time, Pallas kernels for 0%

profile of v1, /device:TPU:0, one launch (start us, length us, event | category | flops | bytes accessed | tf_op | source)
XLA Modules:
  0.0 550.7 jit_solution(15543789882807994988)
XLA Ops:
  6.6 2.0 convert_reduce_fusion
  11.3 2.0 copy.58
  13.3 1.9 slice_bitcast_fusion
  15.2 16.2 %while.28 = (s32[]{:T(128)}, bf16[3,1,256,80]{2,3,1,0:T(8,128)(2,1)}, s32[3]{0:T(128)S(1)}, s32[768]{0:T(1024)S(1)}, bf16[1,768,80]{2,1,0:T(8,128)(2,1)}, /*inde...) while((s32[]{:T(128)}, ...), condition=%wide.region_10.11_spmd, body=%wide.region_7.10_spmd.sunk | while | flops 64527876 | bytes 2797211 | solution.py:92
  32.5 3.5 fusion.81
  36.0 7.2 %all-to-all-start = ((f32[16,48,1280]{2,1,0:T(8,128)}), f32[16,48,1280]{2,1,0:T(8,128)}, u32[]{:S(2)}, u32[]{:S(2)}) async-start(f32[16,48,1280]{2,1,0:T(8,128)} %fusion.81), calls=%async_computation | async-start | bytes 7864320 | tf_op jit(solution)/shard_map/all_to_all | solution.py:29
  43.2 59.5 %all-to-all-done = f32[16,48,1280]{2,1,0:T(8,128)} async-done(((f32[16,48,1280]{2,1,0:T(8,128)}), f32[16,48,1280]{2,1,0:T(8,128)}, u32[]{:S(2)}, u32[]{:S(2)}) %all-to-all-start) | async-done | bytes 3932192 | tf_op jit(solution)/shard_map/all_to_all | solution.py:29
  102.7 2.3 reduce_sum.97
  107.9 4.5 all-to-all-start.1
  115.6 24.9 %all-to-all-done.1 = bf16[16,48,1280]{2,1,0:T(8,128)(2,1)} async-done(((bf16[16,48,1280]{2,1,0:T(8,128)(2,1)}), bf16[16,48,1280]{2,1,0:T(8,128)(2,1)}, u32[]{:S(2)}, u32[]{:S(2)}) %all-to-all-start.1) | async-done | bytes 1966112 | tf_op jit(solution)/shard_map/all_to_all | solution.py:41
  140.5 4.1 reshape_reshape.3
  144.6 3.6 fusion.68
  149.3 5.3 all-to-all-start.2
  154.7 17.3 %all-to-all-done.2 = bf16[8,192,320]{2,1,0:T(8,128)(2,1)S(1)} async-done(((bf16[8,192,320]{2,1,0:T(8,128)(2,1)}), bf16[8,192,320]{2,1,0:T(8,128)(2,1)S(1)}, u32[]{:S(2)}, u32[]{:S(2)}) %all-to-all-start.2) | async-done | bytes 983072 | tf_op jit(solution)/shard_map/all_to_all | solution.py:41
  171.9 11.0 %gather_fusion = bf16[3072,320]{1,0:T(8,128)(2,1)S(1)} fusion(bf16[1536,320]{1,0:T(8,128)(2,1)S(1)} %bitcast.152, s32[3072]{0:T(1024)S(1)} %broadcast_clamp_fusion), kind=kCustom, calls=%fused_computation | custom fusion | bytes 3944448 | tf_op jit(solution)/shard_map/jit(_take)/gather | solution.py:159
  182.9 7.6 %fusion.49 = f32[3072,1024]{1,0:T(8,128)} fusion(bf16[320,1024]{1,0:T(8,128)(2,1)} %param.28, bf16[3072,320]{1,0:T(8,128)(2,1)S(1)} %gather_fusion, pred[3072]{0:T(1024)(128)(4,1)} %compare_and_fusion.1, pred[3072]{0:T(1024)(128)(4,1)S(1)} %ge.77), kind=kOutput, calls=%fused_computation.63 | convolution fusion | flops 2015232000 | bytes 15210496 | tf_op jit(solution)/shard_map/dot_general | solution.py:162
  192.1 88.8 %reduce-scatter.2.cloned.1.call-done = f32[192,1024]{1,0:T(8,128)} async-done(((f32[3072,1024]{1,0:T(8,128)}), f32[192,1024]{1,0:T(8,128)}) %reduce-scatter.2.cloned.1.call-update) | async-done | bytes 786448 | tf_op jit(solution)/shard_map/reduce_scatter | solution.py:161
  282.1 2.1 gather_fusion.1
  284.7 9.6 %all_to_all.27 = f32[8,1,384]{2,1,0:T(1,128)S(1)} all-to-all(f32[8,1,384]{2,1,0:T(1,128)S(1)} %broadcast_in_dim.162), channel_id=1, replica_groups=mesh['enc'=8,'ctx'=16] {'enc'}, dimensions={0} | all-to-all | bytes 24576 | tf_op jit(solution)/shard_map/all_to_all | solution.py:41
  294.3 3.5 tile.2
  297.8 4.7 all-to-all-start.3
  302.6 72.0 %all-to-all-done.3 = bf16[384,8,1024]{2,0,1:T(8,128)(2,1)} async-done(((bf16[384,8,1024]{2,0,1:T(8,128)(2,1)}), bf16[384,8,1024]{2,0,1:T(8,128)(2,1)}, u32[]{:S(2)}, u32[]{:S(2)}) %all-to-all-start.3) | async-done | bytes 6291488 | tf_op jit(solution)/shard_map/all_to_all | solution.py:16
  374.6 8.6 %copy.60 = bf16[384,8,1024]{0,2,1:T(8,128)(2,1)} copy(bf16[384,8,1024]{2,0,1:T(8,128)(2,1)} %all-to-all-done.3) | data formatting | bytes 12582912 | tf_op jit(solution)/shard_map/all_to_all | solution.py:16
  383.3 5.6 %fusion.42 = bf16[384,8192]{0,1:T(8,128)(2,1)S(1)} fusion(bf16[384,8,1024]{0,2,1:T(8,128)(2,1)} %copy.60, f32[8192]{0:T(1024)S(1)} %copy-done.6, f32[384]{0:T(512)S(1)} %add_rsqrt_fusion.1), kind=kLoop, calls=%fused_computation.52 | loop fusion | flops 12582912 | bytes 12617216 | tf_op jit(solution)/shard_map/convert_element_type | solution.py:180
  398.1 8.8 %convolution_convert_fusion = bf16[384,512]{1,0:T(8,128)(2,1)S(1)} fusion(bf16[384,8192]{0,1:T(8,128)(2,1)} %copy-done.2, bf16[8192,512]{1,0:T(8,128)(2,1)} %param.33), kind=kOutput, calls=%fused_computation.73 | convolution fusion | flops 3221422080 | bytes 15073280 | tf_op jit(solution)/shard_map/dot_general | solution.py:181
  407.8 35.1 %all-gather.2.cloned.1.call-done = bf16[6144,256]{0,1:T(8,128)(2,1)} async-done(((bf16[384,256]{0,1:T(8,128)(2,1)}), bf16[6144,256]{0,1:T(8,128)(2,1)}) %all-gather.2.cloned.1.call-update) | async-done | bytes 3145744 | tf_op jit(solution)/shard_map/all_gather | solution.py:55
  442.9 98.2 %conditional.1 = (f32[1,4,384]{2,1,0:T(4,128)}, f32[1,4,384,128]{3,2,1,0:T(8,128)}) conditional(s32[]{:T(128)} %convert_element_type.78, () %tuple.31, (bf16[6144,256]{0,1:T(8,128)(2,1)}, s32[]{:T(128)}, s32[384]{0:T(512)S(1)}, s32[6144]{0:T(1024)}, s32[384]{0:T(512)S(1)}, /*index=5*/bf16[1,4,384,128]{3,2,1,0:T(8,128)(2,1)}) %tuple.87), branch_computations={%region_17.18_spmd, %region_18.23_spmd} | conditional | flops 412493696 | bytes 25149788 | solution.py:244
  442.9 3.2 copy.63
  446.1 1.9 fusion.89
  448.0 93.2 %while.27 = (s32[]{:T(128)}, f32[1,4,384]{2,1,0:T(4,128)S(1)}, f32[1,4,384]{2,1,0:T(4,128)}, f32[1,4,384,128]{3,2,1,0:T(8,128)}, s32[384]{0:T(512)S(1)}, /*index...) while((s32[]{:T(128)}, f32[1,4,384]{2,1,0:T(4,128)S(1)}, ...), condition=%wide.region_22.22_spmd.clone, body=%wide.region_19.21_spmd.clone.sunk | while | flops 412493312 | bytes 12563663 | solution.py:239
  450.7 2.8 fusion.121
  457.6 3.1 fusion.121
  463.7 1.7 fusion.118
  465.4 3.1 fusion.121
  471.5 1.7 fusion.118
  473.3 3.1 fusion.121
  479.4 1.7 fusion.118
  481.1 3.1 fusion.121
  487.2 1.7 fusion.118
  489.0 3.1 fusion.121
  495.1 1.7 fusion.118
  496.8 3.1 fusion.121
  502.9 1.7 fusion.118
  504.7 3.1 fusion.121
  512.5 3.1 fusion.121
  520.4 3.1 fusion.121
  528.2 3.1 fusion.121
  536.1 3.1 fusion.121
  (199 shorter events, 81.0 us)
Async XLA Ops:
  6.5 138.1 %copy-start = (bf16[5120,320]{0,1:T(8,128)(2,1)S(1)}, bf16[5120,320]{0,1:T(8,128)(2,1)}, u32[]{:S(2)}) copy-start(bf16[5120,320]{0,1:T(8,128)(2,1)} %param.27) | copy-start | bytes 9830404
  6.5 3.0 copy-start.12
  6.5 2.3 copy-start.3
  6.5 3.0 copy-start.11
  9.5 5.7 %copy-start.8 = (s32[768]{0:T(1024)S(1)}, s32[768]{0:T(1024)}, u32[]{:S(2)}) copy-start(s32[768]{0:T(1024)} %param.22) | copy-start | bytes 9220
  36.0 66.7 %all-to-all-start = ((f32[16,48,1280]{2,1,0:T(8,128)}), f32[16,48,1280]{2,1,0:T(8,128)}, u32[]{:S(2)}, u32[]{:S(2)}) async-start(f32[16,48,1280]{2,1,0:T(8,128)} %fusion.81), calls=%async_computation | async-start | bytes 7864320 | tf_op jit(solution)/shard_map/all_to_all | solution.py:29
  43.2 63.2 %copy-start.7 = (f32[1280]{0:T(1024)S(1)}, f32[1280]{0:T(1024)}, u32[]{:S(2)}) copy-start(f32[1280]{0:T(1024)} %param.26) | copy-start | bytes 15364
  106.3 6.0 %copy-start.5 = (s32[6144]{0:T(1024)S(1)}, s32[6144]{0:T(1024)}, u32[]{:S(2)}) copy-start(s32[6144]{0:T(1024)} %param.30) | copy-start | bytes 73732
  107.9 32.7 %all-to-all-start.1 = ((bf16[16,48,1280]{2,1,0:T(8,128)(2,1)}), bf16[16,48,1280]{2,1,0:T(8,128)(2,1)}, u32[]{:S(2)}, u32[]{:S(2)}) async-start(bf16[16,48,1280]{2,1,0:T(8,128)(2,1)} %broadcast_in_dim.157), calls=%async_computation.1 | async-start | bytes 3932160 | tf_op jit(solution)/shard_map/all_to_all | solution.py:41
  149.3 22.6 %all-to-all-start.2 = ((bf16[8,192,320]{2,1,0:T(8,128)(2,1)}), bf16[8,192,320]{2,1,0:T(8,128)(2,1)S(1)}, u32[]{:S(2)}, u32[]{:S(2)}) async-start(bf16[8,192,320]{2,1,0:T(8,128)(2,1)} %broadcast_in_dim.158), calls=%async_computation.2 | async-start | bytes 2359296 | tf_op jit(solution)/shard_map/all_to_all | solution.py:41
  154.6 126.3 %reduce-scatter.2.cloned.1.call-start = ((), (), s32[]{:S(2)}) async-start(), calls=%async_computation.6 | async-start | bytes 13369344 | tf_op jit(solution)/shard_map/reduce_scatter | solution.py:161
  282.1 2.1 copy-start.4
  297.8 76.9 %all-to-all-start.3 = ((bf16[384,8,1024]{2,0,1:T(8,128)(2,1)}), bf16[384,8,1024]{2,0,1:T(8,128)(2,1)}, u32[]{:S(2)}, u32[]{:S(2)}) async-start(bf16[384,8,1024]{2,0,1:T(8,128)(2,1)} %tile.2), calls=%async_computation.4 | async-start | bytes 12582912 | tf_op jit(solution)/shard_map/all_to_all | solution.py:16
  302.5 140.4 %all-gather.2.cloned.1.call-start = ((), (), s32[]{:S(2)}) async-start(), calls=%async_computation.7 | async-start | bytes 3342336 | tf_op jit(solution)/shard_map/all_gather | solution.py:55
  302.6 80.6 %copy-start.6 = (f32[8192]{0:T(1024)S(1)}, f32[8192]{0:T(1024)}, u32[]{:S(2)}) copy-start(f32[8192]{0:T(1024)} %param.32) | copy-start | bytes 98308
  383.3 5.6 %copy-start.9 = (bf16[8192,128]{1,0:T(8,128)(2,1)S(1)}, bf16[8192,128]{1,0:T(8,128)(2,1)}, u32[]{:S(2)}) copy-start(bf16[8192,128]{1,0:T(8,128)(2,1)} %param.35) | copy-start | bytes 6291460
  388.9 2.9 copy-start.2
  388.9 3.2 copy-start.10
  541.2 2.7 copy-start.1
Sparse Core Ops, SparseCore 0:
  190.7 90.1 reduce-scatter.1
  394.2 48.6 all-gather.1
